TPU v7x, 32 devices: a whole 2x2x4 slice. The times are simulated.
32 devices in a mesh: rows: 32 (over z, y, x, core).
Axes of the slice: x: 2, y: 2, z: 4, core: 2. Of those that a mesh axis runs over, the one named last changes fastest.
Arguments:
- start_panel: float32 [8, 32768], P(None, 'rows'), may hold values from -10 to 10, as said below
- diagonal_inverse: bfloat16 [32, 1024, 1024], P('rows'), may hold values from -0.6 to 12.5
- right_factor: bfloat16 [32, 1024, 1024], P('rows'), may hold values from -0.03125 to 0.03125
- left_factor: bfloat16 [32, 1024, 1024], P('rows'), may hold values from -0.03125 to 0.03125
Outputs:
- new_panels: float32 [24, 32768], P(None, 'rows')
- coefficients: float32 [3, 32, 8], replicated
- first_coefficients: float32 [3, 32, 8], replicated
Inputs may be any that keep to these rules, and one draw needn't show every extreme that they name: The rows of start_panel are orthonormal under the inner product divided by 32768, up to float32 rounding.
All inputs are finite; a program needn't handle non-finite values.
Results may differ from a plain program's by a relative error of at most 0.014.
Values sent between devices are 32-bit elements; how exact they have to be, the bound alone decides.
A program may use at most 64 MiB of HBM per device.

v0:
```python
import jax
import jax.numpy as jnp
from jax import lax
from jax.sharding import PartitionSpec as P

STEPS = 3
BASIS = 32


epsilon = 1e-06


def passed_along(value, axis, steps):
    count = lax.axis_size(axis)
    initial, last = (max(0, -steps), min(count, count - steps))
    return lax.ppermute(value, axis, [(source, source + steps) for source in range(initial, last)])


def cyclic_solve(current, diagonal_inverse, right_factor, left_factor):
    levels = lax.axis_size("rows").bit_length() - 1
    updated = current
    for height in range(levels):
        distance = 2**height
        lowered = updated.astype(jnp.bfloat16)
        upward = jnp.dot(lowered, right_factor[0], preferred_element_type=jnp.float32)
        downward = jnp.dot(lowered, left_factor[0], preferred_element_type=jnp.float32)
        from_below = passed_along(upward, "rows", distance)
        from_above = passed_along(downward, "rows", -distance)
        updated = updated - from_below - from_above
    return jnp.dot(
        updated.astype(jnp.bfloat16), diagonal_inverse[0], preferred_element_type=jnp.float32
    )


def product(left, right):
    return jnp.dot(left, right, precision=lax.Precision.HIGHEST)


def inner_rows(left, right):
    return jnp.dot(left, right.T, precision=lax.Precision.HIGHEST)


def extend_gram(previous, cross_gram, width):
    if previous is None:
        return cross_gram
    upper = jnp.concatenate([previous, cross_gram[:-width]], 1)
    return jnp.concatenate([upper, cross_gram.T], 0)


def body(start_panel, diagonal_inverse, right_factor, left_factor):
    width = start_panel.shape[0]
    unknowns = start_panel.shape[1] * lax.axis_size("rows")
    krylov_basis = start_panel
    current = start_panel
    gram_basis = None
    produced = []
    coefficients = []
    firsts = []
    for iteration in range(STEPS):
        images = cyclic_solve(current, diagonal_inverse, right_factor, left_factor)
        height = krylov_basis.shape[0]
        reduced = lax.psum(
            (
                inner_rows(krylov_basis, images),
                inner_rows(krylov_basis, current),
                inner_rows(images, images),
            ),
            "rows",
        )
        coef_first = reduced[0] / unknowns
        gram_basis = extend_gram(gram_basis, reduced[1] / unknowns, width)
        coef_second = coef_first - product(gram_basis, coef_first)
        combined = coef_first + coef_second
        remainder = images - product(combined.T, krylov_basis)
        gram_new = (
            reduced[2] / unknowns
            - product(combined.T, coef_first)
            - product(coef_first.T, combined)
        )
        gram_new = gram_new + product(combined.T, product(gram_basis, combined))
        gram_new = gram_new + epsilon * jnp.eye(width, dtype=jnp.float32)
        lower_factor = jnp.linalg.cholesky(gram_new)
        fresh = jax.scipy.linalg.solve_triangular(lower_factor, remainder, lower=True)
        column_block = jnp.zeros((BASIS, width), jnp.float32)
        column_block = column_block.at[:height].set(combined)
        column_block = column_block.at[height : height + width].set(lower_factor.T)
        first_block = jnp.zeros((BASIS, width), jnp.float32).at[:height].set(coef_first)
        produced.append(fresh)
        coefficients.append(column_block)
        firsts.append(first_block)
        krylov_basis = jnp.concatenate([krylov_basis, fresh], 0)
        current = fresh
    return (jnp.concatenate(produced, 0), jnp.stack(coefficients), jnp.stack(firsts))


def solution(mesh):
    return jax.shard_map(
        body,
        mesh=mesh,
        in_specs=(
            P(None, "rows"),
            P("rows", None, None),
            P("rows", None, None),
            P("rows", None, None),
        ),
        out_specs=(P(None, "rows"), P(), P()),
        check_vma=False,
    )
```

profile of v0, /device:TPU:0, one launch (start us, length us, event | category | flops | bytes accessed | tf_op | source)
XLA Modules:
  0.0 292.7 jit_solution(507729210778719122)
XLA Ops:
  0.7 2.1 fusion.64
  2.8 2.5 collective-permute-start
  7.0 3.9 %collective-permute-done.1 = f32[8,1024]{1,0:T(8,128)S(1)} collective-permute-done((f32[8,1024]{1,0:T(8,128)S(1)}, f32[8,1024]{1,0:T(8,128)S(1)}, u32[]{:S(2)}, u32[]{:S(2)}) %collective-permute-start.1) | collective-permute-done | bytes 32800 | tf_op jit(solution)/shard_map/ppermute | solution.py:16
  11.7 4.4 %collective-permute-start.2 = (f32[8,1024]{1,0:T(8,128)S(1)}, f32[8,1024]{1,0:T(8,128)S(1)}, u32[]{:S(2)}, u32[]{:S(2)}) collective-permute-start(f32[8,1024]{1,0:T(8,128)S(1)} %fusion.62), channel_id=1, source_target_pairs={{0,2},{1,3},{2,4},{3,5},{4,6},{5,7},{6,8},{7,9},{8,10},{9,11},{10,... | collective-permute-start | bytes 98312 | tf_op jit(solution)/shard_map/ppermute | solution.py:16
  17.7 4.6 %collective-permute-done.3 = f32[8,1024]{1,0:T(8,128)S(1)} collective-permute-done((f32[8,1024]{1,0:T(8,128)S(1)}, f32[8,1024]{1,0:T(8,128)S(1)}, u32[]{:S(2)}, u32[]{:S(2)}) %collective-permute-start.3) | collective-permute-done | bytes 32800 | tf_op jit(solution)/shard_map/ppermute | solution.py:16
  23.1 4.3 %collective-permute-start.4 = (f32[8,1024]{1,0:T(8,128)S(1)}, f32[8,1024]{1,0:T(8,128)S(1)}, u32[]{:S(2)}, u32[]{:S(2)}) collective-permute-start(f32[8,1024]{1,0:T(8,128)S(1)} %fusion.60), channel_id=1, source_target_pairs={{0,4},{1,5},{2,6},{3,7},{4,8},{5,9},{6,10},{7,11},{8,12},{9,13},{1... | collective-permute-start | bytes 98312 | tf_op jit(solution)/shard_map/ppermute | solution.py:16
  29.0 4.3 %collective-permute-done.5 = f32[8,1024]{1,0:T(8,128)S(1)} collective-permute-done((f32[8,1024]{1,0:T(8,128)S(1)}, f32[8,1024]{1,0:T(8,128)S(1)}, u32[]{:S(2)}, u32[]{:S(2)}) %collective-permute-start.5) | collective-permute-done | bytes 32800 | tf_op jit(solution)/shard_map/ppermute | solution.py:16
  34.1 3.5 %collective-permute-start.6 = (f32[8,1024]{1,0:T(8,128)S(1)}, f32[8,1024]{1,0:T(8,128)S(1)}, u32[]{:S(2)}, u32[]{:S(2)}) collective-permute-start(f32[8,1024]{1,0:T(8,128)S(1)} %fusion.58), channel_id=1, source_target_pairs={{0,8},{1,9},{2,10},{3,11},{4,12},{5,13},{6,14},{7,15},{8,16},{9,17... | collective-permute-start | bytes 98312 | tf_op jit(solution)/shard_map/ppermute | solution.py:16
  39.1 4.2 %collective-permute-done.7 = f32[8,1024]{1,0:T(8,128)S(1)} collective-permute-done((f32[8,1024]{1,0:T(8,128)S(1)}, f32[8,1024]{1,0:T(8,128)S(1)}, u32[]{:S(2)}, u32[]{:S(2)}) %collective-permute-start.7) | collective-permute-done | bytes 32800 | tf_op jit(solution)/shard_map/ppermute | solution.py:16
  44.1 4.1 %collective-permute-start.8 = (f32[8,1024]{1,0:T(8,128)S(1)}, f32[8,1024]{1,0:T(8,128)S(1)}, u32[]{:S(2)}, u32[]{:S(2)}) collective-permute-start(f32[8,1024]{1,0:T(8,128)S(1)} %fusion.56), channel_id=1, source_target_pairs={{0,16},{1,17},{2,18},{3,19},{4,20},{5,21},{6,22},{7,23},{8,24},{9,... | collective-permute-start | bytes 98312 | tf_op jit(solution)/shard_map/ppermute | solution.py:16
  49.8 5.1 %collective-permute-done.9 = f32[8,1024]{1,0:T(8,128)S(1)} collective-permute-done((f32[8,1024]{1,0:T(8,128)S(1)}, f32[8,1024]{1,0:T(8,128)S(1)}, u32[]{:S(2)}, u32[]{:S(2)}) %collective-permute-start.9) | collective-permute-done | bytes 32800 | tf_op jit(solution)/shard_map/ppermute | solution.py:16
  55.6 39.3 %all-reduce.8 = (f32[8,8]{0,1:T(8,128)S(1)}, f32[8,8]{0,1:T(8,128)S(1)}, f32[8,8]{0,1:T(8,128)S(1)}) all-reduce(f32[8,8]{0,1:T(8,128)S(1)} %fusion.143, f32[8,8]{0,1:T(8,128)S(1)} %convolution_bitcast_fusion, f32[8,8]{0,1:T(8,128)S(1)} %fusion.142), channel_id=1, replica_groups=mesh['rows'=32] {'rows'}, use_global_device_ids=true, to_apply=%region_2.0 | all-reduce | flops 192 | bytes 1536 | tf_op jit(solution)/shard_map/psum | solution.py:62
  103.3 4.3 %collective-permute-done.11 = f32[8,1024]{1,0:T(8,128)S(1)} collective-permute-done((f32[8,1024]{1,0:T(8,128)S(1)}, f32[8,1024]{1,0:T(8,128)S(1)}, u32[]{:S(2)}, u32[]{:S(2)}) %collective-permute-start.11) | collective-permute-done | bytes 32800 | tf_op jit(solution)/shard_map/ppermute | solution.py:16
  108.3 4.4 %collective-permute-start.12 = (f32[8,1024]{1,0:T(8,128)S(1)}, f32[8,1024]{1,0:T(8,128)S(1)}, u32[]{:S(2)}, u32[]{:S(2)}) collective-permute-start(f32[8,1024]{1,0:T(8,128)S(1)} %fusion.52), channel_id=1, source_target_pairs={{0,2},{1,3},{2,4},{3,5},{4,6},{5,7},{6,8},{7,9},{8,10},{9,11},{10,... | collective-permute-start | bytes 98312 | tf_op jit(solution)/shard_map/ppermute | solution.py:16
  114.3 4.6 %collective-permute-done.13 = f32[8,1024]{1,0:T(8,128)S(1)} collective-permute-done((f32[8,1024]{1,0:T(8,128)S(1)}, f32[8,1024]{1,0:T(8,128)S(1)}, u32[]{:S(2)}, u32[]{:S(2)}) %collective-permute-start.13) | collective-permute-done | bytes 32800 | tf_op jit(solution)/shard_map/ppermute | solution.py:16
  119.7 4.1 %collective-permute-start.14 = (f32[8,1024]{1,0:T(8,128)S(1)}, f32[8,1024]{1,0:T(8,128)S(1)}, u32[]{:S(2)}, u32[]{:S(2)}) collective-permute-start(f32[8,1024]{1,0:T(8,128)S(1)} %fusion.50), channel_id=1, source_target_pairs={{0,4},{1,5},{2,6},{3,7},{4,8},{5,9},{6,10},{7,11},{8,12},{9,13},{1... | collective-permute-start | bytes 98312 | tf_op jit(solution)/shard_map/ppermute | solution.py:16
  125.4 4.3 %collective-permute-done.15 = f32[8,1024]{1,0:T(8,128)S(1)} collective-permute-done((f32[8,1024]{1,0:T(8,128)S(1)}, f32[8,1024]{1,0:T(8,128)S(1)}, u32[]{:S(2)}, u32[]{:S(2)}) %collective-permute-start.15) | collective-permute-done | bytes 32800 | tf_op jit(solution)/shard_map/ppermute | solution.py:16
  130.4 3.1 %collective-permute-start.16 = (f32[8,1024]{1,0:T(8,128)S(1)}, f32[8,1024]{1,0:T(8,128)S(1)}, u32[]{:S(2)}, u32[]{:S(2)}) collective-permute-start(f32[8,1024]{1,0:T(8,128)S(1)} %fusion.48), channel_id=1, source_target_pairs={{0,8},{1,9},{2,10},{3,11},{4,12},{5,13},{6,14},{7,15},{8,16},{9,17... | collective-permute-start | bytes 98312 | tf_op jit(solution)/shard_map/ppermute | solution.py:16
  135.1 4.2 %collective-permute-done.17 = f32[8,1024]{1,0:T(8,128)S(1)} collective-permute-done((f32[8,1024]{1,0:T(8,128)S(1)}, f32[8,1024]{1,0:T(8,128)S(1)}, u32[]{:S(2)}, u32[]{:S(2)}) %collective-permute-start.17) | collective-permute-done | bytes 32800 | tf_op jit(solution)/shard_map/ppermute | solution.py:16
  140.1 2.0 collective-permute-start.18
  143.7 5.1 %collective-permute-done.19 = f32[8,1024]{1,0:T(8,128)S(1)} collective-permute-done((f32[8,1024]{1,0:T(8,128)S(1)}, f32[8,1024]{1,0:T(8,128)S(1)}, u32[]{:S(2)}, u32[]{:S(2)}) %collective-permute-start.19) | collective-permute-done | bytes 32800 | tf_op jit(solution)/shard_map/ppermute | solution.py:16
  149.5 39.8 %all-reduce.7 = (f32[16,8]{1,0:T(8,128)S(1)}, f32[16,8]{1,0:T(8,128)S(1)}, f32[8,8]{0,1:T(8,128)S(1)}) all-reduce(f32[16,8]{1,0:T(8,128)S(1)} %fusion.72, f32[16,8]{1,0:T(8,128)S(1)} %fusion.73, f32[8,8]{0,1:T(8,128)S(1)} %fusion.144), channel_id=1, replica_groups=mesh['rows'=32] {'rows'}, use_global_device_ids=true, to_apply=%region_7.0 | all-reduce | flops 320 | bytes 2560 | tf_op jit(solution)/shard_map/psum | solution.py:62
  198.4 4.1 %collective-permute-done.21 = f32[8,1024]{1,0:T(8,128)S(1)} collective-permute-done((f32[8,1024]{1,0:T(8,128)S(1)}, f32[8,1024]{1,0:T(8,128)S(1)}, u32[]{:S(2)}, u32[]{:S(2)}) %collective-permute-start.21) | collective-permute-done | bytes 32800 | tf_op jit(solution)/shard_map/ppermute | solution.py:16
  203.3 4.4 %collective-permute-start.22 = (f32[8,1024]{1,0:T(8,128)S(1)}, f32[8,1024]{1,0:T(8,128)S(1)}, u32[]{:S(2)}, u32[]{:S(2)}) collective-permute-start(f32[8,1024]{1,0:T(8,128)S(1)} %fusion.42), channel_id=1, source_target_pairs={{0,2},{1,3},{2,4},{3,5},{4,6},{5,7},{6,8},{7,9},{8,10},{9,11},{10,... | collective-permute-start | bytes 98312 | tf_op jit(solution)/shard_map/ppermute | solution.py:16
  209.3 4.6 %collective-permute-done.23 = f32[8,1024]{1,0:T(8,128)S(1)} collective-permute-done((f32[8,1024]{1,0:T(8,128)S(1)}, f32[8,1024]{1,0:T(8,128)S(1)}, u32[]{:S(2)}, u32[]{:S(2)}) %collective-permute-start.23) | collective-permute-done | bytes 32800 | tf_op jit(solution)/shard_map/ppermute | solution.py:16
  214.7 4.0 %collective-permute-start.24 = (f32[8,1024]{1,0:T(8,128)S(1)}, f32[8,1024]{1,0:T(8,128)S(1)}, u32[]{:S(2)}, u32[]{:S(2)}) collective-permute-start(f32[8,1024]{1,0:T(8,128)S(1)} %fusion.40), channel_id=1, source_target_pairs={{0,4},{1,5},{2,6},{3,7},{4,8},{5,9},{6,10},{7,11},{8,12},{9,13},{1... | collective-permute-start | bytes 98312 | tf_op jit(solution)/shard_map/ppermute | solution.py:16
  220.2 4.3 %collective-permute-done.25 = f32[8,1024]{1,0:T(8,128)S(1)} collective-permute-done((f32[8,1024]{1,0:T(8,128)S(1)}, f32[8,1024]{1,0:T(8,128)S(1)}, u32[]{:S(2)}, u32[]{:S(2)}) %collective-permute-start.25) | collective-permute-done | bytes 32800 | tf_op jit(solution)/shard_map/ppermute | solution.py:16
  225.3 3.1 %collective-permute-start.26 = (f32[8,1024]{1,0:T(8,128)S(1)}, f32[8,1024]{1,0:T(8,128)S(1)}, u32[]{:S(2)}, u32[]{:S(2)}) collective-permute-start(f32[8,1024]{1,0:T(8,128)S(1)} %fusion.38), channel_id=1, source_target_pairs={{0,8},{1,9},{2,10},{3,11},{4,12},{5,13},{6,14},{7,15},{8,16},{9,17... | collective-permute-start | bytes 98312 | tf_op jit(solution)/shard_map/ppermute | solution.py:16
  229.9 4.2 %collective-permute-done.27 = f32[8,1024]{1,0:T(8,128)S(1)} collective-permute-done((f32[8,1024]{1,0:T(8,128)S(1)}, f32[8,1024]{1,0:T(8,128)S(1)}, u32[]{:S(2)}, u32[]{:S(2)}) %collective-permute-start.27) | collective-permute-done | bytes 32800 | tf_op jit(solution)/shard_map/ppermute | solution.py:16
  235.0 2.0 collective-permute-start.28
  238.5 5.1 %collective-permute-done.29 = f32[8,1024]{1,0:T(8,128)S(1)} collective-permute-done((f32[8,1024]{1,0:T(8,128)S(1)}, f32[8,1024]{1,0:T(8,128)S(1)}, u32[]{:S(2)}, u32[]{:S(2)}) %collective-permute-start.29) | collective-permute-done | bytes 32800 | tf_op jit(solution)/shard_map/ppermute | solution.py:16
  246.0 40.0 %all-reduce.6 = (f32[24,8]{1,0:T(8,128)S(1)}, f32[24,8]{1,0:T(8,128)S(1)}, f32[8,8]{0,1:T(8,128)S(1)}) all-reduce(f32[24,8]{1,0:T(8,128)S(1)} %fusion.75, f32[24,8]{1,0:T(8,128)S(1)} %fusion.74, f32[8,8]{0,1:T(8,128)S(1)} %fusion.145), channel_id=1, replica_groups=mesh['rows'=32] {'rows'}, use_global_device_ids=true, to_apply=%region_9.0 | all-reduce | flops 448 | bytes 3584 | tf_op jit(solution)/shard_map/psum | solution.py:62
  (171 shorter events, 57.5 us)
Async XLA Ops:
  2.8 4.2 %collective-permute-start = (f32[8,1024]{1,0:T(8,128)S(1)}, f32[8,1024]{1,0:T(8,128)S(1)}, u32[]{:S(2)}, u32[]{:S(2)}) collective-permute-start(f32[8,1024]{1,0:T(8,128)S(1)} %fusion.64), channel_id=1, source_target_pairs={{0,1},{1,2},{2,3},{3,4},{4,5},{5,6},{6,7},{7,8},{8,9},{9,10},{10,1... | collective-permute-start | bytes 98312 | tf_op jit(solution)/shard_map/ppermute | solution.py:16
  5.7 5.2 %collective-permute-start.1 = (f32[8,1024]{1,0:T(8,128)S(1)}, f32[8,1024]{1,0:T(8,128)S(1)}, u32[]{:S(2)}, u32[]{:S(2)}) collective-permute-start(f32[8,1024]{1,0:T(8,128)S(1)} %fusion.34), channel_id=1, source_target_pairs={{1,0},{2,1},{3,2},{4,3},{5,4},{6,5},{7,6},{8,7},{9,8},{10,9},{11,1... | collective-permute-start | bytes 98312 | tf_op jit(solution)/shard_map/ppermute | solution.py:16
  11.7 6.0 %collective-permute-start.2 = (f32[8,1024]{1,0:T(8,128)S(1)}, f32[8,1024]{1,0:T(8,128)S(1)}, u32[]{:S(2)}, u32[]{:S(2)}) collective-permute-start(f32[8,1024]{1,0:T(8,128)S(1)} %fusion.62), channel_id=1, source_target_pairs={{0,2},{1,3},{2,4},{3,5},{4,6},{5,7},{6,8},{7,9},{8,10},{9,11},{10,... | collective-permute-start | bytes 98312 | tf_op jit(solution)/shard_map/ppermute | solution.py:16
  16.1 6.2 %collective-permute-start.3 = (f32[8,1024]{1,0:T(8,128)S(1)}, f32[8,1024]{1,0:T(8,128)S(1)}, u32[]{:S(2)}, u32[]{:S(2)}) collective-permute-start(f32[8,1024]{1,0:T(8,128)S(1)} %fusion.32), channel_id=1, source_target_pairs={{2,0},{3,1},{4,2},{5,3},{6,4},{7,5},{8,6},{9,7},{10,8},{11,9},{12,... | collective-permute-start | bytes 98312 | tf_op jit(solution)/shard_map/ppermute | solution.py:16
  23.1 5.9 %collective-permute-start.4 = (f32[8,1024]{1,0:T(8,128)S(1)}, f32[8,1024]{1,0:T(8,128)S(1)}, u32[]{:S(2)}, u32[]{:S(2)}) collective-permute-start(f32[8,1024]{1,0:T(8,128)S(1)} %fusion.60), channel_id=1, source_target_pairs={{0,4},{1,5},{2,6},{3,7},{4,8},{5,9},{6,10},{7,11},{8,12},{9,13},{1... | collective-permute-start | bytes 98312 | tf_op jit(solution)/shard_map/ppermute | solution.py:16
  27.4 5.9 %collective-permute-start.5 = (f32[8,1024]{1,0:T(8,128)S(1)}, f32[8,1024]{1,0:T(8,128)S(1)}, u32[]{:S(2)}, u32[]{:S(2)}) collective-permute-start(f32[8,1024]{1,0:T(8,128)S(1)} %fusion.30), channel_id=1, source_target_pairs={{4,0},{5,1},{6,2},{7,3},{8,4},{9,5},{10,6},{11,7},{12,8},{13,9},{1... | collective-permute-start | bytes 98312 | tf_op jit(solution)/shard_map/ppermute | solution.py:16
  34.1 5.1 %collective-permute-start.6 = (f32[8,1024]{1,0:T(8,128)S(1)}, f32[8,1024]{1,0:T(8,128)S(1)}, u32[]{:S(2)}, u32[]{:S(2)}) collective-permute-start(f32[8,1024]{1,0:T(8,128)S(1)} %fusion.58), channel_id=1, source_target_pairs={{0,8},{1,9},{2,10},{3,11},{4,12},{5,13},{6,14},{7,15},{8,16},{9,17... | collective-permute-start | bytes 98312 | tf_op jit(solution)/shard_map/ppermute | solution.py:16
  37.5 5.8 %collective-permute-start.7 = (f32[8,1024]{1,0:T(8,128)S(1)}, f32[8,1024]{1,0:T(8,128)S(1)}, u32[]{:S(2)}, u32[]{:S(2)}) collective-permute-start(f32[8,1024]{1,0:T(8,128)S(1)} %fusion.28), channel_id=1, source_target_pairs={{8,0},{9,1},{10,2},{11,3},{12,4},{13,5},{14,6},{15,7},{16,8},{17,9... | collective-permute-start | bytes 98312 | tf_op jit(solution)/shard_map/ppermute | solution.py:16
  43.4 11.6 %copy-start.6 = (bf16[1,1024,1024]{2,1,0:T(8,128)(2,1)S(1)}, bf16[1,1024,1024]{2,1,0:T(8,128)(2,1)}, u32[]{:S(2)}) copy-start(bf16[1,1024,1024]{2,1,0:T(8,128)(2,1)} %param.26) | copy-start | bytes 6291460
  44.1 5.7 %collective-permute-start.8 = (f32[8,1024]{1,0:T(8,128)S(1)}, f32[8,1024]{1,0:T(8,128)S(1)}, u32[]{:S(2)}, u32[]{:S(2)}) collective-permute-start(f32[8,1024]{1,0:T(8,128)S(1)} %fusion.56), channel_id=1, source_target_pairs={{0,16},{1,17},{2,18},{3,19},{4,20},{5,21},{6,22},{7,23},{8,24},{9,... | collective-permute-start | bytes 98312 | tf_op jit(solution)/shard_map/ppermute | solution.py:16
  48.2 6.7 %collective-permute-start.9 = (f32[8,1024]{1,0:T(8,128)S(1)}, f32[8,1024]{1,0:T(8,128)S(1)}, u32[]{:S(2)}, u32[]{:S(2)}) collective-permute-start(f32[8,1024]{1,0:T(8,128)S(1)} %fusion.26), channel_id=1, source_target_pairs={{16,0},{17,1},{18,2},{19,3},{20,4},{21,5},{22,6},{23,7},{24,8},{25... | collective-permute-start | bytes 98312 | tf_op jit(solution)/shard_map/ppermute | solution.py:16
  100.7 2.6 collective-permute-start.10
  101.9 5.6 %collective-permute-start.11 = (f32[8,1024]{1,0:T(8,128)S(1)}, f32[8,1024]{1,0:T(8,128)S(1)}, u32[]{:S(2)}, u32[]{:S(2)}) collective-permute-start(f32[8,1024]{1,0:T(8,128)S(1)} %fusion.24), channel_id=1, source_target_pairs={{1,0},{2,1},{3,2},{4,3},{5,4},{6,5},{7,6},{8,7},{9,8},{10,9},{11,1... | collective-permute-start | bytes 98312 | tf_op jit(solution)/shard_map/ppermute | solution.py:16
  108.3 6.0 %collective-permute-start.12 = (f32[8,1024]{1,0:T(8,128)S(1)}, f32[8,1024]{1,0:T(8,128)S(1)}, u32[]{:S(2)}, u32[]{:S(2)}) collective-permute-start(f32[8,1024]{1,0:T(8,128)S(1)} %fusion.52), channel_id=1, source_target_pairs={{0,2},{1,3},{2,4},{3,5},{4,6},{5,7},{6,8},{7,9},{8,10},{9,11},{10,... | collective-permute-start | bytes 98312 | tf_op jit(solution)/shard_map/ppermute | solution.py:16
  112.8 6.2 %collective-permute-start.13 = (f32[8,1024]{1,0:T(8,128)S(1)}, f32[8,1024]{1,0:T(8,128)S(1)}, u32[]{:S(2)}, u32[]{:S(2)}) collective-permute-start(f32[8,1024]{1,0:T(8,128)S(1)} %fusion.22), channel_id=1, source_target_pairs={{2,0},{3,1},{4,2},{5,3},{6,4},{7,5},{8,6},{9,7},{10,8},{11,9},{12,... | collective-permute-start | bytes 98312 | tf_op jit(solution)/shard_map/ppermute | solution.py:16
  119.7 5.7 %collective-permute-start.14 = (f32[8,1024]{1,0:T(8,128)S(1)}, f32[8,1024]{1,0:T(8,128)S(1)}, u32[]{:S(2)}, u32[]{:S(2)}) collective-permute-start(f32[8,1024]{1,0:T(8,128)S(1)} %fusion.50), channel_id=1, source_target_pairs={{0,4},{1,5},{2,6},{3,7},{4,8},{5,9},{6,10},{7,11},{8,12},{9,13},{1... | collective-permute-start | bytes 98312 | tf_op jit(solution)/shard_map/ppermute | solution.py:16
  123.8 5.9 %collective-permute-start.15 = (f32[8,1024]{1,0:T(8,128)S(1)}, f32[8,1024]{1,0:T(8,128)S(1)}, u32[]{:S(2)}, u32[]{:S(2)}) collective-permute-start(f32[8,1024]{1,0:T(8,128)S(1)} %fusion.20), channel_id=1, source_target_pairs={{4,0},{5,1},{6,2},{7,3},{8,4},{9,5},{10,6},{11,7},{12,8},{13,9},{1... | collective-permute-start | bytes 98312 | tf_op jit(solution)/shard_map/ppermute | solution.py:16
  130.4 4.6 %collective-permute-start.16 = (f32[8,1024]{1,0:T(8,128)S(1)}, f32[8,1024]{1,0:T(8,128)S(1)}, u32[]{:S(2)}, u32[]{:S(2)}) collective-permute-start(f32[8,1024]{1,0:T(8,128)S(1)} %fusion.48), channel_id=1, source_target_pairs={{0,8},{1,9},{2,10},{3,11},{4,12},{5,13},{6,14},{7,15},{8,16},{9,17... | collective-permute-start | bytes 98312 | tf_op jit(solution)/shard_map/ppermute | solution.py:16
  133.5 5.8 %collective-permute-start.17 = (f32[8,1024]{1,0:T(8,128)S(1)}, f32[8,1024]{1,0:T(8,128)S(1)}, u32[]{:S(2)}, u32[]{:S(2)}) collective-permute-start(f32[8,1024]{1,0:T(8,128)S(1)} %fusion.18), channel_id=1, source_target_pairs={{8,0},{9,1},{10,2},{11,3},{12,4},{13,5},{14,6},{15,7},{16,8},{17,9... | collective-permute-start | bytes 98312 | tf_op jit(solution)/shard_map/ppermute | solution.py:16
  139.3 9.5 %copy-start.7 = (bf16[1,1024,1024]{2,1,0:T(8,128)(2,1)S(1)}, bf16[1,1024,1024]{2,1,0:T(8,128)(2,1)}, u32[]{:S(2)}) copy-start(bf16[1,1024,1024]{2,1,0:T(8,128)(2,1)} %param.26) | copy-start | bytes 6291460
  140.1 3.6 %collective-permute-start.18 = (f32[8,1024]{1,0:T(8,128)S(1)}, f32[8,1024]{1,0:T(8,128)S(1)}, u32[]{:S(2)}, u32[]{:S(2)}) collective-permute-start(f32[8,1024]{1,0:T(8,128)S(1)} %fusion.46), channel_id=1, source_target_pairs={{0,16},{1,17},{2,18},{3,19},{4,20},{5,21},{6,22},{7,23},{8,24},{9,... | collective-permute-start | bytes 98312 | tf_op jit(solution)/shard_map/ppermute | solution.py:16
  142.1 6.7 %collective-permute-start.19 = (f32[8,1024]{1,0:T(8,128)S(1)}, f32[8,1024]{1,0:T(8,128)S(1)}, u32[]{:S(2)}, u32[]{:S(2)}) collective-permute-start(f32[8,1024]{1,0:T(8,128)S(1)} %fusion.16), channel_id=1, source_target_pairs={{16,0},{17,1},{18,2},{19,3},{20,4},{21,5},{22,6},{23,7},{24,8},{25... | collective-permute-start | bytes 98312 | tf_op jit(solution)/shard_map/ppermute | solution.py:16
  195.6 2.8 collective-permute-start.20
  196.9 5.6 %collective-permute-start.21 = (f32[8,1024]{1,0:T(8,128)S(1)}, f32[8,1024]{1,0:T(8,128)S(1)}, u32[]{:S(2)}, u32[]{:S(2)}) collective-permute-start(f32[8,1024]{1,0:T(8,128)S(1)} %fusion.14), channel_id=1, source_target_pairs={{1,0},{2,1},{3,2},{4,3},{5,4},{6,5},{7,6},{8,7},{9,8},{10,9},{11,1... | collective-permute-start | bytes 98312 | tf_op jit(solution)/shard_map/ppermute | solution.py:16
  203.3 6.1 %collective-permute-start.22 = (f32[8,1024]{1,0:T(8,128)S(1)}, f32[8,1024]{1,0:T(8,128)S(1)}, u32[]{:S(2)}, u32[]{:S(2)}) collective-permute-start(f32[8,1024]{1,0:T(8,128)S(1)} %fusion.42), channel_id=1, source_target_pairs={{0,2},{1,3},{2,4},{3,5},{4,6},{5,7},{6,8},{7,9},{8,10},{9,11},{10,... | collective-permute-start | bytes 98312 | tf_op jit(solution)/shard_map/ppermute | solution.py:16
  207.7 6.2 %collective-permute-start.23 = (f32[8,1024]{1,0:T(8,128)S(1)}, f32[8,1024]{1,0:T(8,128)S(1)}, u32[]{:S(2)}, u32[]{:S(2)}) collective-permute-start(f32[8,1024]{1,0:T(8,128)S(1)} %fusion.12), channel_id=1, source_target_pairs={{2,0},{3,1},{4,2},{5,3},{6,4},{7,5},{8,6},{9,7},{10,8},{11,9},{12,... | collective-permute-start | bytes 98312 | tf_op jit(solution)/shard_map/ppermute | solution.py:16
  214.7 5.5 %collective-permute-start.24 = (f32[8,1024]{1,0:T(8,128)S(1)}, f32[8,1024]{1,0:T(8,128)S(1)}, u32[]{:S(2)}, u32[]{:S(2)}) collective-permute-start(f32[8,1024]{1,0:T(8,128)S(1)} %fusion.40), channel_id=1, source_target_pairs={{0,4},{1,5},{2,6},{3,7},{4,8},{5,9},{6,10},{7,11},{8,12},{9,13},{1... | collective-permute-start | bytes 98312 | tf_op jit(solution)/shard_map/ppermute | solution.py:16
  218.7 5.9 %collective-permute-start.25 = (f32[8,1024]{1,0:T(8,128)S(1)}, f32[8,1024]{1,0:T(8,128)S(1)}, u32[]{:S(2)}, u32[]{:S(2)}) collective-permute-start(f32[8,1024]{1,0:T(8,128)S(1)} %fusion.10), channel_id=1, source_target_pairs={{4,0},{5,1},{6,2},{7,3},{8,4},{9,5},{10,6},{11,7},{12,8},{13,9},{1... | collective-permute-start | bytes 98312 | tf_op jit(solution)/shard_map/ppermute | solution.py:16
  225.3 4.6 %collective-permute-start.26 = (f32[8,1024]{1,0:T(8,128)S(1)}, f32[8,1024]{1,0:T(8,128)S(1)}, u32[]{:S(2)}, u32[]{:S(2)}) collective-permute-start(f32[8,1024]{1,0:T(8,128)S(1)} %fusion.38), channel_id=1, source_target_pairs={{0,8},{1,9},{2,10},{3,11},{4,12},{5,13},{6,14},{7,15},{8,16},{9,17... | collective-permute-start | bytes 98312 | tf_op jit(solution)/shard_map/ppermute | solution.py:16
  228.4 5.8 %collective-permute-start.27 = (f32[8,1024]{1,0:T(8,128)S(1)}, f32[8,1024]{1,0:T(8,128)S(1)}, u32[]{:S(2)}, u32[]{:S(2)}) collective-permute-start(f32[8,1024]{1,0:T(8,128)S(1)} %fusion.8), channel_id=1, source_target_pairs={{8,0},{9,1},{10,2},{11,3},{12,4},{13,5},{14,6},{15,7},{16,8},{17,9... | collective-permute-start | bytes 98312 | tf_op jit(solution)/shard_map/ppermute | solution.py:16
  235.0 3.6 %collective-permute-start.28 = (f32[8,1024]{1,0:T(8,128)S(1)}, f32[8,1024]{1,0:T(8,128)S(1)}, u32[]{:S(2)}, u32[]{:S(2)}) collective-permute-start(f32[8,1024]{1,0:T(8,128)S(1)} %fusion.36), channel_id=1, source_target_pairs={{0,16},{1,17},{2,18},{3,19},{4,20},{5,21},{6,22},{7,23},{8,24},{9,... | collective-permute-start | bytes 98312 | tf_op jit(solution)/shard_map/ppermute | solution.py:16
  237.0 6.7 %collective-permute-start.29 = (f32[8,1024]{1,0:T(8,128)S(1)}, f32[8,1024]{1,0:T(8,128)S(1)}, u32[]{:S(2)}, u32[]{:S(2)}) collective-permute-start(f32[8,1024]{1,0:T(8,128)S(1)} %fusion.6), channel_id=1, source_target_pairs={{16,0},{17,1},{18,2},{19,3},{20,4},{21,5},{22,6},{23,7},{24,8},{25... | collective-permute-start | bytes 98312 | tf_op jit(solution)/shard_map/ppermute | solution.py:16
  (7 other events, 30.9 us)
where the time goes:
time: 294 us; the launch traced here: 293 us
  blocking collectives  119 us (40%)
  waiting for transfers between devices  69.3 us (24%)
  starting transfers between devices  67.9 us (23%)
  matrix products  22.1 us (8%)
  other arithmetic  10 us (3%)
  local copies, waits for them, and re-layouts  3.09 us (1%)
    psum x3, blocking collectives, body(): lax.psum((inner_rows(krylov_basis, images), inner_rows(krylov_basis, curr...  119 us
    ppermute x30, waiting for transfers between devices, passed_along(): lax.ppermute(value, axis, [(source, source + steps) for source in range(i...  69.3 us
    ppermute x30, starting transfers between devices, passed_along(): lax.ppermute(value, axis, [(source, source + steps) for source in range(i...  67.9 us
    dot_general x15, matrix products, cyclic_solve(): jnp.dot(lowered, right_factor[0], preferred_element_type=jnp.float32)  7.53 us
  transfers between devices with their start and end apart: 30, of which 26 were waited for; matrix products, arithmetic and copies ran while one was open for 0% of the time, Pallas kernels for 0%

commit v1 on v0

v1 whole, which is shorter than its diff:
```python
import functools

import jax
import jax.numpy as jnp
from jax import lax
from jax.experimental import pallas as pl
from jax.experimental.pallas import tpu as pltpu
from jax.sharding import PartitionSpec as P

STEPS = 3
BASIS = 32
LANES = 128
AXIS = "rows"
MESH = pl.DeviceIdType.MESH

epsilon = 1e-06


def radixes_of(count):
    sizes = []
    while count > 1:
        size = 8 if count >= 8 else count
        sizes.append(size)
        count //= size
    return sizes


def product(left, right):
    return jnp.dot(left, right, precision=lax.Precision.HIGHEST, preferred_element_type=jnp.float32)


def inner_rows(left, right):
    return lax.dot_general(
        left,
        right,
        (((1,), (1,)), ((), ())),
        precision=lax.Precision.HIGHEST,
        preferred_element_type=jnp.float32,
    )


def kernel(
    n,
    start_ref,
    diagonal_hbm,
    right_hbm,
    left_hbm,
    panels_ref,
    coef_ref,
    first_ref,
    right_w,
    left_w,
    diagonal_w,
    vectors,
    gram,
    outgoing,
    incoming,
    tiles,
    load_sem,
    send_sem,
    recv_sem,
    tile_send,
    tile_recv,
):
    me = lax.axis_index(AXIS)
    width, block = start_ref.shape
    depth = vectors.shape[0]
    unknowns = block * n
    levels = n.bit_length() - 1
    groups = []
    stride, offset = 1, 0
    for size in radixes_of(n):
        groups.append((size, stride, offset))
        stride, offset = stride * size, offset + size

    loads = [
        pltpu.make_async_copy(source.at[0], target, load_sem.at[i])
        for i, (source, target) in enumerate(
            ((right_hbm, right_w), (left_hbm, left_w), (diagonal_hbm, diagonal_w))
        )
    ]
    for load in loads:
        load.start()

    barrier = pltpu.get_barrier_semaphore()
    expected = 0
    for level in range(levels):
        distance = 2**level
        for target, present in (
            (me + distance, me + distance < n),
            (me - distance, me >= distance),
        ):
            @pl.when(present)
            def _():
                pl.semaphore_signal(barrier, inc=1, device_id=(target,), device_id_type=MESH)

            expected = expected + present.astype(jnp.int32)
    for size, stride, _ in groups:
        digit = (me // stride) % size
        for k in range(1, size):
            partner = me + ((digit + k) % size - digit) * stride
            pl.semaphore_signal(barrier, inc=1, device_id=(partner,), device_id_type=MESH)
        expected = expected + (size - 1)

    vectors[...] = jnp.zeros_like(vectors)
    vectors[pl.ds(width, width), :] = start_ref[...]
    gram[...] = jnp.zeros_like(gram)

    row = lax.broadcasted_iota(jnp.int32, (depth, depth), 0)
    col = lax.broadcasted_iota(jnp.int32, (depth, depth), 1)
    eye = (row == col).astype(jnp.float32)
    below = col < (row // width) * width
    basis_lane = lax.broadcasted_iota(jnp.int32, (width, depth), 1) >= width
    small_row = lax.broadcasted_iota(jnp.int32, (width, width), 0)
    small_col = lax.broadcasted_iota(jnp.int32, (width, width), 1)
    small_eye = (small_row == small_col).astype(jnp.float32)
    column_row = lax.broadcasted_iota(jnp.int32, (width, 1), 0)

    def widened(value):
        return jnp.concatenate(
            [value, jnp.zeros((value.shape[0], LANES - value.shape[1]), jnp.float32)], 1
        )

    def row_copy(step, level, way):
        distance = 2**level
        return pltpu.make_async_remote_copy(
            src_ref=outgoing.at[step, level, way],
            dst_ref=incoming.at[step, level, way],
            send_sem=send_sem.at[step, level, way],
            recv_sem=recv_sem.at[step, level, way],
            device_id=(me + distance if way == 0 else me - distance,),
            device_id_type=MESH,
        )

    def sends(level, way):
        distance = 2**level
        return me + distance < n if way == 0 else me >= distance

    def receives(level, way):
        return sends(level, 1 - way)

    def tile_copies(step, kind, phase):
        size, stride, offset = groups[phase]
        digit = (me // stride) % size
        copies = []
        for k in range(1, size):
            other = (digit + k) % size
            copies.append(
                pltpu.make_async_remote_copy(
                    src_ref=tiles.at[step, kind, offset + digit],
                    dst_ref=tiles.at[step, kind, offset + digit],
                    send_sem=tile_send.at[step, kind, offset + k],
                    recv_sem=tile_recv.at[step, kind, offset + digit],
                    device_id=(me + (other - digit) * stride,),
                    device_id_type=MESH,
                )
            )
        return copies

    def tile_start(step, kind, phase, value):
        size, stride, offset = groups[phase]
        digit = (me // stride) % size
        tiles[step, kind, offset + digit] = value
        for copy in tile_copies(step, kind, phase):
            copy.start()

    def tile_finish(step, kind, phase):
        size, stride, offset = groups[phase]
        digit = (me // stride) % size
        for k in range(1, size):
            other = (digit + k) % size
            pltpu.make_async_remote_copy(
                src_ref=tiles.at[step, kind, offset + digit],
                dst_ref=tiles.at[step, kind, offset + other],
                send_sem=tile_send.at[step, kind, offset + k],
                recv_sem=tile_recv.at[step, kind, offset + other],
                device_id=(me + (other - digit) * stride,),
                device_id_type=MESH,
            ).wait_recv()
        total = tiles[step, kind, offset]
        for i in range(1, size):
            total = total + tiles[step, kind, offset + i]
        return total

    loads[0].wait()
    loads[1].wait()
    loads[2].wait()
    pl.semaphore_wait(barrier, expected)

    def arnoldi_step(step, current):
        updated = current
        pending = 0
        total = None
        for level in range(levels):
            lowered = updated.astype(jnp.bfloat16)
            for way, weights in ((0, right_w), (1, left_w)):
                outgoing[step, level, way] = jnp.dot(
                    lowered, weights[...], preferred_element_type=jnp.float32
                )

                @pl.when(sends(level, way))
                def _():
                    row_copy(step, level, way).start()

            if level == 0:
                tile_start(step, 0, 0, widened(inner_rows(current, vectors[...])))
            elif pending < len(groups):
                total = tile_finish(step, 0, pending)
                pending += 1
                if pending < len(groups):
                    tile_start(step, 0, pending, total)

            for way in range(2):
                @pl.when(receives(level, way))
                def _():
                    row_copy(step, level, way).wait_recv()

                @pl.when(jnp.logical_not(receives(level, way)))
                def _():
                    incoming[step, level, way] = jnp.zeros((width, block), jnp.float32)

            updated = updated - incoming[step, level, 0] - incoming[step, level, 1]
        while pending < len(groups):
            total = tile_finish(step, 0, pending)
            pending += 1
            if pending < len(groups):
                tile_start(step, 0, pending, total)

        images = jnp.dot(
            updated.astype(jnp.bfloat16), diagonal_w[...], preferred_element_type=jnp.float32
        )
        vectors[pl.ds(0, width), :] = images
        tile_start(step, 1, 0, widened(inner_rows(images, vectors[...])))

        cross = total[:, :depth] * (1.0 / unknowns)
        cross = jnp.where(basis_lane, cross, 0.0)
        gram[pl.ds(pl.multiple_of(width * (step + 1), width), width), :] = cross
        lower = gram[...]
        full = lower + inner_rows(eye, jnp.where(below, lower, 0.0))
        excess = full - eye
        both = eye - excess
        inside = both + product(product(excess, excess), both)

        for phase in range(len(groups)):
            reduced = tile_finish(step, 1, phase)
            if phase + 1 < len(groups):
                tile_start(step, 1, phase + 1, reduced)
        reduced = reduced[:, :depth] * (1.0 / unknowns)
        coef_first = jnp.where(basis_lane, reduced, 0.0)
        combined = product(coef_first, both)
        square = (
            reduced[:, :width]
            - inner_rows(product(coef_first, inside), coef_first)
            + epsilon * small_eye
        )
        fresh = images - product(combined, vectors[...])
        factor = jnp.zeros((width, width), jnp.float32)
        for k in range(width):
            inverse = lax.rsqrt(square[k : k + 1, k : k + 1])
            column = square[:, k : k + 1] * inverse
            factor = jnp.where((small_col == k) & (small_row >= k), column, factor)
            column = jnp.where(column_row > k, column, 0.0)
            square_row = square[k : k + 1, :] * inverse
            fresh_row = fresh[k : k + 1, :] * inverse
            square = jnp.where(column_row == k, square_row, square - column * square_row)
            fresh = jnp.where(column_row == k, fresh_row, fresh - column * fresh_row)

        panels_ref[pl.ds(pl.multiple_of(width * step, width), width), :] = fresh
        first_ref[step] = widened(coef_first)
        coef_ref[step] = widened(combined) + pltpu.roll(
            widened(factor), width * (step + 2), 1
        )

        @pl.when(step + 1 < STEPS)
        def _():
            vectors[pl.ds(pl.multiple_of(width * (step + 2), width), width), :] = fresh

        for level in range(levels):
            for way in range(2):
                @pl.when(sends(level, way))
                def _():
                    row_copy(step, level, way).wait_send()
        for kind in range(2):
            for phase in range(len(groups)):
                for copy in tile_copies(step, kind, phase):
                    copy.wait_send()
        return fresh

    lax.fori_loop(0, STEPS, arnoldi_step, start_ref[...])


def body(start_panel, diagonal_inverse, right_factor, left_factor):
    n = lax.axis_size(AXIS)
    width, block = start_panel.shape
    depth = width * (STEPS + 1)
    levels = n.bit_length() - 1
    slots = sum(radixes_of(n))
    dma = pltpu.SemaphoreType.DMA
    any_space = pl.BlockSpec(memory_space=pl.ANY)
    in_vmem = pl.BlockSpec(memory_space=pltpu.VMEM)
    panels, coefs, firsts = pl.pallas_call(
        functools.partial(kernel, n),
        out_shape=(
            jax.ShapeDtypeStruct((width * STEPS, block), jnp.float32),
            jax.ShapeDtypeStruct((STEPS, width, LANES), jnp.float32),
            jax.ShapeDtypeStruct((STEPS, width, LANES), jnp.float32),
        ),
        in_specs=[in_vmem, any_space, any_space, any_space],
        out_specs=(in_vmem, in_vmem, in_vmem),
        scratch_shapes=[
            pltpu.VMEM((block, block), jnp.bfloat16),
            pltpu.VMEM((block, block), jnp.bfloat16),
            pltpu.VMEM((block, block), jnp.bfloat16),
            pltpu.VMEM((depth, block), jnp.float32),
            pltpu.VMEM((depth, depth), jnp.float32),
            pltpu.VMEM((STEPS, levels, 2, width, block), jnp.float32),
            pltpu.VMEM((STEPS, levels, 2, width, block), jnp.float32),
            pltpu.VMEM((STEPS, 2, slots, width, LANES), jnp.float32),
            dma((3,)),
            dma((STEPS, levels, 2)),
            dma((STEPS, levels, 2)),
            dma((STEPS, 2, slots)),
            dma((STEPS, 2, slots)),
        ],
        compiler_params=pltpu.CompilerParams(collective_id=0, has_side_effects=True),
    )(start_panel, diagonal_inverse, right_factor, left_factor)
    shown = slice(width, width + BASIS)
    return (
        panels,
        jnp.transpose(coefs[:, :, shown], (0, 2, 1)),
        jnp.transpose(firsts[:, :, shown], (0, 2, 1)),
    )


def solution(mesh):
    return jax.shard_map(
        body,
        mesh=mesh,
        in_specs=(
            P(None, AXIS),
            P(AXIS, None, None),
            P(AXIS, None, None),
            P(AXIS, None, None),
        ),
        out_specs=(P(None, AXIS), P(), P()),
        check_vma=False,
    )
```

time: 294 us -> 94.7 us (0.32)
  blocking collectives: 119 us -> 0 us
  Pallas kernels: 0 us -> 90.8 us
  waiting for transfers between devices: 69.3 us -> 0 us
  starting transfers between devices: 67.9 us -> 0 us
  matrix products: 22.1 us -> 0 us
  other arithmetic: 10 us -> 0 us
    psum x3 -> x0, blocking collectives: 119 us -> none  [body(): lax.psum((inner_rows(krylov_basis, images), inner_rows(krylov_basis, curr...]
    pallas_call x0 -> x1, Pallas kernels: none -> 90.8 us  [body(): pl.pallas_call(functools.partial(kernel, n), out_shape=(jax.ShapeDtypeStr...]
    ppermute x30 -> x0, waiting for transfers between devices: 69.3 us -> none  [passed_along(): lax.ppermute(value, axis, [(source, source + steps) for source in range(i...]
    ppermute x30 -> x0, starting transfers between devices: 67.9 us -> none  [passed_along(): lax.ppermute(value, axis, [(source, source + steps) for source in range(i...]
    dot_general x60 -> x0, matrix products: 21.4 us -> none  [the longest x15 7.53 us: cyclic_solve(): jnp.dot(lowered, right_factor[0], preferred_element_type=jnp.float32)]
    another operation x18 -> x0, other arithmetic: 9.25 us -> none  [the longest x9 4.22 us: body(): lower_factor = jnp.linalg.cholesky(gram_new)]
  transfers between devices with their start and end apart: 30 -> 0, of which waited for: 26 -> 0; matrix products, arithmetic and copies ran while one was open for 0% -> 0% of each run, Pallas kernels for 0% -> 0%
where the time goes in v1:
time: 94.7 us; the launch traced here: 94.4 us
  Pallas kernels  90.8 us (96%)
  local copies, waits for them, and re-layouts  2.94 us (3%)
    pallas_call x1, Pallas kernels, body(): pl.pallas_call(functools.partial(kernel, n), out_shape=(jax.ShapeDtypeStr...  90.8 us

profile of v1, /device:TPU:0, one launch (start us, length us, event | category | flops | bytes accessed | tf_op | source)
XLA Modules:
  0.0 94.4 jit_solution(18247096094717243756)
XLA Ops:
  0.6 90.8 %shard_map.67 = (f32[24,1024]{1,0:T(8,128)}, f32[3,8,128]{2,1,0:T(8,128)}, f32[3,8,128]{2,1,0:T(8,128)}) custom-call(f32[8,1024]{1,0:T(8,128)} %start_ref.1, bf16[1,1024,1024]{2,1,0:T(8,128)(2,1)} %diagonal_hbm.1, bf16[1,1024,1024]{2,1,0:T(8,128)(2,1)} %right_hbm.1, bf16[1,1024,1024]{2,1,0:T(8,128)(2,1)} %left_hbm.1), custom_call_target="tpu_custom_call" | custom-call | tf_op jit(solution)/shard_map/pallas_call | solution.py:301
  91.5 1.4 %slice_bitcast_fusion = (f32[3,32,8]{1,2,0:T(8,128)}, f32[3,32,8]{1,2,0:T(8,128)}) fusion(f32[3,8,128]{2,1,0:T(8,128)} %get-tuple-element.8, f32[3,8,128]{2,1,0:T(8,128)} %get-tuple-element.7), kind=kLoop, calls=%fused_computation | loop fusion | bytes 12288 | tf_op jit(solution)/shard_map/transpose | solution.py:331
  92.9 1.5 %copy.8 = f32[24,1024]{1,0:T(8,128)} copy(f32[24,1024]{1,0:T(8,128)} %get-tuple-element.14) | data formatting | bytes 196608

commit v2 on v1

--- a/solution.py
+++ b/solution.py
@@ -65,6 +65,7 @@
     me = lax.axis_index(AXIS)
     width, block = start_ref.shape
     depth = vectors.shape[0]
+    half = block // 2
     unknowns = block * n
     levels = n.bit_length() - 1
     groups = []
@@ -114,20 +115,21 @@
     small_row = lax.broadcasted_iota(jnp.int32, (width, width), 0)
     small_col = lax.broadcasted_iota(jnp.int32, (width, width), 1)
     small_eye = (small_row == small_col).astype(jnp.float32)
-    column_row = lax.broadcasted_iota(jnp.int32, (width, 1), 0)
+    tile_row = lax.broadcasted_iota(jnp.int32, (width, LANES), 0)
+    tile_col = lax.broadcasted_iota(jnp.int32, (width, LANES), 1)
 
     def widened(value):
         return jnp.concatenate(
             [value, jnp.zeros((value.shape[0], LANES - value.shape[1]), jnp.float32)], 1
         )
 
-    def row_copy(step, level, way):
+    def row_copy(step, level, way, part):
         distance = 2**level
         return pltpu.make_async_remote_copy(
-            src_ref=outgoing.at[step, level, way],
-            dst_ref=incoming.at[step, level, way],
-            send_sem=send_sem.at[step, level, way],
-            recv_sem=recv_sem.at[step, level, way],
+            src_ref=outgoing.at[step, level, way, part],
+            dst_ref=incoming.at[step, level, way, part],
+            send_sem=send_sem.at[step, level, way, part],
+            recv_sem=recv_sem.at[step, level, way, part],
             device_id=(me + distance if way == 0 else me - distance,),
             device_id_type=MESH,
         )
@@ -182,52 +184,84 @@
             total = total + tiles[step, kind, offset + i]
         return total
 
+    def received(step, level, way, part):
+        @pl.when(receives(level, way))
+        def _():
+            row_copy(step, level, way, part).wait_recv()
+
+        @pl.when(jnp.logical_not(receives(level, way)))
+        def _():
+            incoming[step, level, way, part] = jnp.zeros((width, half), jnp.float32)
+
+    def columns(part):
+        return slice(part * half, (part + 1) * half)
+
+    def partial(lowered, weights, depth_part, part):
+        return jnp.dot(
+            lowered,
+            weights[columns(depth_part), columns(part)],
+            preferred_element_type=jnp.float32,
+        )
+
     loads[0].wait()
     loads[1].wait()
-    loads[2].wait()
     pl.semaphore_wait(barrier, expected)
 
     def arnoldi_step(step, current):
-        updated = current
+        updated = [current[:, columns(part)] for part in range(2)]
         pending = 0
         total = None
+
+        def lowered_part(level, part):
+            if level > 0:
+                for way in range(2):
+                    received(step, level - 1, way, part)
+                updated[part] = (
+                    updated[part]
+                    - incoming[step, level - 1, 0, part]
+                    - incoming[step, level - 1, 1, part]
+                )
+            return updated[part].astype(jnp.bfloat16)
+
         for level in range(levels):
-            lowered = updated.astype(jnp.bfloat16)
-            for way, weights in ((0, right_w), (1, left_w)):
-                outgoing[step, level, way] = jnp.dot(
-                    lowered, weights[...], preferred_element_type=jnp.float32
-                )
-
-                @pl.when(sends(level, way))
-                def _():
-                    row_copy(step, level, way).start()
+            lowered = lowered_part(level, 0)
+            sums = [
+                [partial(lowered, weights, 0, part) for weights in (right_w, left_w)]
+                for part in range(2)
+            ]
+            lowered = lowered_part(level, 1)
+            for part in range(2):
+                for way, weights in ((0, right_w), (1, left_w)):
+                    outgoing[step, level, way, part] = sums[part][way] + partial(
+                        lowered, weights, 1, part
+                    )
+                for way in range(2):
+                    @pl.when(sends(level, way))
+                    def _():
+                        row_copy(step, level, way, part).start()
 
             if level == 0:
                 tile_start(step, 0, 0, widened(inner_rows(current, vectors[...])))
-            elif pending < len(groups):
+            elif level % 2 == 0 and pending < len(groups):
                 total = tile_finish(step, 0, pending)
                 pending += 1
                 if pending < len(groups):
                     tile_start(step, 0, pending, total)
-
-            for way in range(2):
-                @pl.when(receives(level, way))
-                def _():
-                    row_copy(step, level, way).wait_recv()
-
-                @pl.when(jnp.logical_not(receives(level, way)))
-                def _():
-                    incoming[step, level, way] = jnp.zeros((width, block), jnp.float32)
-
-            updated = updated - incoming[step, level, 0] - incoming[step, level, 1]
         while pending < len(groups):
             total = tile_finish(step, 0, pending)
             pending += 1
             if pending < len(groups):
                 tile_start(step, 0, pending, total)
 
-        images = jnp.dot(
-            updated.astype(jnp.bfloat16), diagonal_w[...], preferred_element_type=jnp.float32
+        @pl.when(step == 0)
+        def _():
+            loads[2].wait()
+
+        lowered = lowered_part(levels, 0)
+        sums = [partial(lowered, diagonal_w, 0, part) for part in range(2)]
+        lowered = lowered_part(levels, 1)
+        images = jnp.concatenate(
+            [sums[part] + partial(lowered, diagonal_w, 1, part) for part in range(2)], 1
         )
         vectors[pl.ds(0, width), :] = images
         tile_start(step, 1, 0, widened(inner_rows(images, vectors[...])))
@@ -254,21 +288,25 @@
             + epsilon * small_eye
         )
         fresh = images - product(combined, vectors[...])
-        factor = jnp.zeros((width, width), jnp.float32)
+        sides = [jnp.broadcast_to(square[:, k : k + 1], (width, LANES)) for k in range(width)]
+        pieces = [fresh[:, at : at + LANES] for at in range(0, block, LANES)]
+        factor = jnp.zeros((width, LANES), jnp.float32)
+        scale = jnp.zeros((width, LANES), jnp.float32)
         for k in range(width):
-            inverse = lax.rsqrt(square[k : k + 1, k : k + 1])
-            column = square[:, k : k + 1] * inverse
-            factor = jnp.where((small_col == k) & (small_row >= k), column, factor)
-            column = jnp.where(column_row > k, column, 0.0)
-            square_row = square[k : k + 1, :] * inverse
-            fresh_row = fresh[k : k + 1, :] * inverse
-            square = jnp.where(column_row == k, square_row, square - column * square_row)
-            fresh = jnp.where(column_row == k, fresh_row, fresh - column * fresh_row)
+            root = lax.rsqrt(jnp.broadcast_to(sides[k][k : k + 1, :], (width, LANES)))
+            column = sides[k] * root
+            factor = jnp.where((tile_col == k) & (tile_row >= k), column, factor)
+            scale = jnp.where(tile_row == k, root, scale)
+            ratio = jnp.where(tile_row > k, column * root, 0.0)
+            for j in range(k + 1, width):
+                sides[j] = sides[j] - ratio * sides[j][k : k + 1, :]
+            pieces = [piece - ratio * piece[k : k + 1, :] for piece in pieces]
+        fresh = jnp.concatenate([piece * scale for piece in pieces], 1)
 
         panels_ref[pl.ds(pl.multiple_of(width * step, width), width), :] = fresh
         first_ref[step] = widened(coef_first)
         coef_ref[step] = widened(combined) + pltpu.roll(
-            widened(factor), width * (step + 2), 1
+            factor, width * (step + 2), 1
         )
 
         @pl.when(step + 1 < STEPS)
@@ -279,7 +317,8 @@
             for way in range(2):
                 @pl.when(sends(level, way))
                 def _():
-                    row_copy(step, level, way).wait_send()
+                    for part in range(2):
+                        row_copy(step, level, way, part).wait_send()
         for kind in range(2):
             for phase in range(len(groups)):
                 for copy in tile_copies(step, kind, phase):
@@ -313,12 +352,12 @@
             pltpu.VMEM((block, block), jnp.bfloat16),
             pltpu.VMEM((depth, block), jnp.float32),
             pltpu.VMEM((depth, depth), jnp.float32),
-            pltpu.VMEM((STEPS, levels, 2, width, block), jnp.float32),
-            pltpu.VMEM((STEPS, levels, 2, width, block), jnp.float32),
+            pltpu.VMEM((STEPS, levels, 2, 2, width, block // 2), jnp.float32),
+            pltpu.VMEM((STEPS, levels, 2, 2, width, block // 2), jnp.float32),
             pltpu.VMEM((STEPS, 2, slots, width, LANES), jnp.float32),
             dma((3,)),
-            dma((STEPS, levels, 2)),
-            dma((STEPS, levels, 2)),
+            dma((STEPS, levels, 2, 2)),
+            dma((STEPS, levels, 2, 2)),
             dma((STEPS, 2, slots)),
             dma((STEPS, 2, slots)),
         ],

time: 94.7 us -> 93.3 us (0.985)
  Pallas kernels: 90.8 us -> 89.4 us
    pallas_call x1, Pallas kernels: 90.8 us -> 89.4 us  [body(): pl.pallas_call(functools.partial(kernel, n), out_shape=(jax.ShapeDtypeStr...]
where the time goes in v2:
time: 93.3 us; the launch traced here: 93 us
  Pallas kernels  89.4 us (96%)
  local copies, waits for them, and re-layouts  2.94 us (3%)
    pallas_call x1, Pallas kernels, body(): pl.pallas_call(functools.partial(kernel, n), out_shape=(jax.ShapeDtypeStr...  89.4 us

profile of v2, /device:TPU:0, one launch (start us, length us, event | category | flops | bytes accessed | tf_op | source)
XLA Modules:
  0.0 93.0 jit_solution(17362790489181261973)
XLA Ops:
  0.6 89.4 %shard_map.67 = (f32[24,1024]{1,0:T(8,128)}, f32[3,8,128]{2,1,0:T(8,128)}, f32[3,8,128]{2,1,0:T(8,128)}) custom-call(f32[8,1024]{1,0:T(8,128)} %start_ref.1, bf16[1,1024,1024]{2,1,0:T(8,128)(2,1)} %diagonal_hbm.1, bf16[1,1024,1024]{2,1,0:T(8,128)(2,1)} %right_hbm.1, bf16[1,1024,1024]{2,1,0:T(8,128)(2,1)} %left_hbm.1), custom_call_target="tpu_custom_call" | custom-call | tf_op jit(solution)/shard_map/pallas_call | solution.py:340
  90.0 1.4 %slice_bitcast_fusion = (f32[3,32,8]{1,2,0:T(8,128)}, f32[3,32,8]{1,2,0:T(8,128)}) fusion(f32[3,8,128]{2,1,0:T(8,128)} %get-tuple-element.8, f32[3,8,128]{2,1,0:T(8,128)} %get-tuple-element.7), kind=kLoop, calls=%fused_computation | loop fusion | bytes 12288 | tf_op jit(solution)/shard_map/transpose | solution.py:370
  91.4 1.5 %copy.8 = f32[24,1024]{1,0:T(8,128)} copy(f32[24,1024]{1,0:T(8,128)} %get-tuple-element.14) | data formatting | bytes 196608

commit v3 on v2

--- a/solution.py
+++ b/solution.py
@@ -10,16 +10,17 @@
 STEPS = 3
 BASIS = 32
 LANES = 128
+GROUPS = (8, 32)
 AXIS = "rows"
 MESH = pl.DeviceIdType.MESH
 
 epsilon = 1e-06
 
 
-def radixes_of(count):
+def radixes_of(count, most):
     sizes = []
     while count > 1:
-        size = 8 if count >= 8 else count
+        size = min(count, most)
         sizes.append(size)
         count //= size
     return sizes
@@ -68,11 +69,14 @@
     half = block // 2
     unknowns = block * n
     levels = n.bit_length() - 1
-    groups = []
-    stride, offset = 1, 0
-    for size in radixes_of(n):
-        groups.append((size, stride, offset))
-        stride, offset = stride * size, offset + size
+    plans = []
+    for most in GROUPS:
+        plan, stride, offset = [], 1, 0
+        for size in radixes_of(n, most):
+            plan.append((size, stride, offset))
+            stride, offset = stride * size, offset + size
+        plans.append(plan)
+    groups = plans[0]
 
     loads = [
         pltpu.make_async_copy(source.at[0], target, load_sem.at[i])
@@ -96,7 +100,7 @@
                 pl.semaphore_signal(barrier, inc=1, device_id=(target,), device_id_type=MESH)
 
             expected = expected + present.astype(jnp.int32)
-    for size, stride, _ in groups:
+    for size, stride, _ in plans[0] + plans[1]:
         digit = (me // stride) % size
         for k in range(1, size):
             partner = me + ((digit + k) % size - digit) * stride
@@ -142,7 +146,7 @@
         return sends(level, 1 - way)
 
     def tile_copies(step, kind, phase):
-        size, stride, offset = groups[phase]
+        size, stride, offset = plans[kind][phase]
         digit = (me // stride) % size
         copies = []
         for k in range(1, size):
@@ -160,14 +164,14 @@
         return copies
 
     def tile_start(step, kind, phase, value):
-        size, stride, offset = groups[phase]
+        size, stride, offset = plans[kind][phase]
         digit = (me // stride) % size
         tiles[step, kind, offset + digit] = value
         for copy in tile_copies(step, kind, phase):
             copy.start()
 
     def tile_finish(step, kind, phase):
-        size, stride, offset = groups[phase]
+        size, stride, offset = plans[kind][phase]
         digit = (me // stride) % size
         for k in range(1, size):
             other = (digit + k) % size
@@ -275,9 +279,9 @@
         both = eye - excess
         inside = both + product(product(excess, excess), both)
 
-        for phase in range(len(groups)):
+        for phase in range(len(plans[1])):
             reduced = tile_finish(step, 1, phase)
-            if phase + 1 < len(groups):
+            if phase + 1 < len(plans[1]):
                 tile_start(step, 1, phase + 1, reduced)
         reduced = reduced[:, :depth] * (1.0 / unknowns)
         coef_first = jnp.where(basis_lane, reduced, 0.0)
@@ -320,7 +324,7 @@
                     for part in range(2):
                         row_copy(step, level, way, part).wait_send()
         for kind in range(2):
-            for phase in range(len(groups)):
+            for phase in range(len(plans[kind])):
                 for copy in tile_copies(step, kind, phase):
                     copy.wait_send()
         return fresh
@@ -333,7 +337,7 @@
     width, block = start_panel.shape
     depth = width * (STEPS + 1)
     levels = n.bit_length() - 1
-    slots = sum(radixes_of(n))
+    slots = max(sum(radixes_of(n, most)) for most in GROUPS)
     dma = pltpu.SemaphoreType.DMA
     any_space = pl.BlockSpec(memory_space=pl.ANY)
     in_vmem = pl.BlockSpec(memory_space=pltpu.VMEM)

time: 93.3 us -> 93.9 us (level)
  no operation moved by 1% of the time
where the time goes in v3:
time: 93.9 us; the launch traced here: 93.6 us
  Pallas kernels  90 us (96%)
  local copies, waits for them, and re-layouts  2.94 us (3%)
    pallas_call x1, Pallas kernels, body(): pl.pallas_call(functools.partial(kernel, n), out_shape=(jax.ShapeDtypeStr...  90 us

profile of v3, /device:TPU:0, one launch (start us, length us, event | category | flops | bytes accessed | tf_op | source)
XLA Modules:
  0.0 93.6 jit_solution(2768844943336301288)
XLA Ops:
  0.6 90.0 %shard_map.67 = (f32[24,1024]{1,0:T(8,128)}, f32[3,8,128]{2,1,0:T(8,128)}, f32[3,8,128]{2,1,0:T(8,128)}) custom-call(f32[8,1024]{1,0:T(8,128)} %start_ref.1, bf16[1,1024,1024]{2,1,0:T(8,128)(2,1)} %diagonal_hbm.1, bf16[1,1024,1024]{2,1,0:T(8,128)(2,1)} %right_hbm.1, bf16[1,1024,1024]{2,1,0:T(8,128)(2,1)} %left_hbm.1), custom_call_target="tpu_custom_call" | custom-call | tf_op jit(solution)/shard_map/pallas_call | solution.py:344
  90.6 1.4 %slice_bitcast_fusion = (f32[3,32,8]{1,2,0:T(8,128)}, f32[3,32,8]{1,2,0:T(8,128)}) fusion(f32[3,8,128]{2,1,0:T(8,128)} %get-tuple-element.8, f32[3,8,128]{2,1,0:T(8,128)} %get-tuple-element.7), kind=kLoop, calls=%fused_computation | loop fusion | bytes 12288 | tf_op jit(solution)/shard_map/transpose | solution.py:374
  92.0 1.5 %copy.8 = f32[24,1024]{1,0:T(8,128)} copy(f32[24,1024]{1,0:T(8,128)} %get-tuple-element.14) | data formatting | bytes 196608
